TPU v7x, 32 devices: a whole 2x2x4 slice. The times are simulated.
32 devices in a mesh: fsdp: 4 (over z), tp: 8 (over y, x, core).
Axes of the slice: x: 2, y: 2, z: 4, core: 2. Of those that a mesh axis runs over, the one named last changes fastest.
Arguments:
- tokens: bfloat16 [3008, 4096], P('fsdp', 'tp'), may hold values from -6 to 6
- norm_gain: float32 [4096], replicated, may hold values from 0.5 to 1.5
- base_gate: bfloat16 [4096, 12288], P(None, 'tp'), may hold values from -0.09375 to 0.09375
- base_up: bfloat16 [4096, 12288], P(None, 'tp'), may hold values from -0.09375 to 0.09375
- base_down: bfloat16 [12288, 4096], P('tp'), may hold values from -0.0546875 to 0.0546875
- code_gate: bfloat16 [4096, 12288], P(('fsdp', 'tp')), may hold values from -4 to 4
- code_up: bfloat16 [4096, 12288], P(('fsdp', 'tp')), may hold values from -4 to 4
- scale_gate: float32 [4096, 96], P(('fsdp', 'tp')), may hold values from 0.005 to 0.05
- scale_up: float32 [4096, 96], P(('fsdp', 'tp')), may hold values from 0.005 to 0.05
- code_down: bfloat16 [12288, 4096], P(None, ('fsdp', 'tp')), may hold values from -4 to 4
- scale_down: float32 [96, 4096], P(None, ('fsdp', 'tp')), may hold values from 0.005 to 0.05
- cu_seqlens: int32 [4, 9], P('fsdp'), may hold values from 0 to 752, as said below
Outputs:
- mixed: bfloat16 [3008, 4096], P('fsdp', 'tp')
- seq_means: float32 [32, 4096], P('fsdp', 'tp')
Inputs may be any that keep to these rules, and one draw needn't show every extreme that they name: `cu_seqlens`: each row starts at 0 and rises strictly; its last entry is the group's live tokens, which fill the first slots of its 752. Over all groups the live tokens add up to exactly 1536, and some group has exactly 752.
All inputs are finite; a program needn't handle non-finite values.
Results may differ from a plain program's by a relative error of at most 0.023.
Values may be sent and summed in bfloat16 or wider, within the bound.
A program may use at most 256 MiB of HBM per device.

v0:
```python
import jax
import jax.numpy as jnp
from jax import lax
from jax.sharding import PartitionSpec as P

SEQS = 8
EPSILON = 1e-06
F32, BF16 = (jnp.float32, jnp.bfloat16)


def dequant_rows(base_part, code_part, scales):
    rows, cols = code_part.shape
    blocks = scales.shape[1]
    delta = code_part.astype(F32).reshape(rows, blocks, cols // blocks) * scales[:, :, None]
    return (base_part.astype(F32) + delta.reshape(rows, cols)).astype(BF16)


def dequant_cols(base_part, code_part, scales):
    rows, cols = code_part.shape
    blocks = scales.shape[0]
    delta = code_part.astype(F32).reshape(blocks, rows // blocks, cols) * scales[:, None, :]
    return (base_part.astype(F32) + delta.reshape(rows, cols)).astype(BF16)


def swap_up(part, axis_name="tp"):
    return lax.all_to_all(part, axis_name, split_axis=1, concat_axis=0, tiled=True)


def swap_down(part):
    return lax.all_to_all(part, "tp", split_axis=0, concat_axis=1, tiled=True)


def shards(
    tokens,
    norm_gain,
    base_gate,
    base_up,
    base_down,
    code_gate,
    code_up,
    scale_gate,
    scale_up,
    code_down,
    scale_down,
    cu_seqlens,
):
    groups = lax.axis_size("fsdp")
    slices = lax.axis_size("tp")
    me_f = lax.axis_index("fsdp")
    me_t = lax.axis_index("tp")
    cap, feat = tokens.shape
    width = base_gate.shape[0]
    depth = width // groups
    units = base_gate.shape[1]
    live_all = groups * (cap // 2 + SEQS)
    grain = 16 * slices
    capp = -(-cap // grain) * grain
    part = capp // slices
    padded = jnp.pad(tokens, ((0, capp - cap), (0, 0)))
    rows_full = lax.all_to_all(padded, "tp", split_axis=0, concat_axis=1, tiled=True)
    wide = rows_full.astype(F32)
    inverse = lax.rsqrt(jnp.mean(wide * wide, axis=1, keepdims=True) + EPSILON)
    normed = (wide * inverse * norm_gain[None, :]).astype(BF16)
    block = swap_up(normed, "fsdp")
    every = lax.all_gather(block, "tp", axis=0, tiled=True)
    bounds_all = lax.all_gather(cu_seqlens, "fsdp", axis=0, tiled=True)
    counts = bounds_all[:, SEQS]
    ends = jnp.cumsum(counts)
    starts = ends - counts
    place = jnp.arange(live_all, dtype=jnp.int32)
    group_of = jnp.sum((place[:, None] >= ends[None, :]).astype(jnp.int32), axis=1)
    group_of = jnp.minimum(group_of, groups - 1)
    slot = place - jnp.take(starts, group_of)
    source = slot // part * (groups * part) + group_of * part + slot % part
    pick = (source[:, None] == jnp.arange(slices * groups * part, dtype=jnp.int32)[None, :]).astype(
        BF16
    )
    packed = jnp.dot(pick, every, preferred_element_type=F32).astype(BF16)
    gate_rows = lax.dynamic_slice_in_dim(base_gate, me_f * depth, depth, 0)
    up_rows = lax.dynamic_slice_in_dim(base_up, me_f * depth, depth, 0)
    w_gate = dequant_rows(gate_rows, swap_up(code_gate), swap_up(scale_gate))
    w_up = dequant_rows(up_rows, swap_up(code_up), swap_up(scale_up))
    gate_part = jnp.dot(packed, w_gate, preferred_element_type=F32).astype(BF16)
    up_part = jnp.dot(packed, w_up, preferred_element_type=F32).astype(BF16)
    up_part, code_down = lax.optimization_barrier((up_part, code_down))
    gate_sum = lax.psum_scatter(gate_part, "fsdp", scatter_dimension=0, tiled=True)
    up_sum = lax.psum_scatter(up_part, "fsdp", scatter_dimension=0, tiled=True)
    down_codes, down_scales = (swap_down(code_down), swap_down(scale_down))
    gate_sum, up_sum, down_codes, down_scales = lax.optimization_barrier(
        (gate_sum, up_sum, down_codes, down_scales)
    )
    hidden = (jax.nn.silu(gate_sum.astype(F32)) * up_sum.astype(F32)).astype(BF16)
    hidden_all = lax.all_gather(hidden, "fsdp", axis=0, tiled=True)
    down_cols = lax.dynamic_slice_in_dim(base_down, me_f * depth, depth, 1)
    w_down = dequant_cols(down_cols, down_codes, down_scales)
    out_part = jnp.dot(hidden_all, w_down, preferred_element_type=F32).astype(BF16)
    out_cols = lax.psum_scatter(out_part, "tp", scatter_dimension=1, tiled=True)
    narrow = out_cols.shape[1]
    grp = jnp.arange(groups, dtype=jnp.int32)
    slots = jnp.arange(cap, dtype=jnp.int32)
    wanted = jnp.where(slots[None, :] < counts[:, None], starts[:, None] + slots[None, :], -1)
    spread = (wanted.reshape(-1)[:, None] == place[None, :]).astype(BF16)
    placed_rows = jnp.dot(spread, out_cols, preferred_element_type=F32).astype(BF16)
    mine = lax.all_to_all(
        placed_rows.reshape(groups, cap, narrow), "fsdp", split_axis=0, concat_axis=0, tiled=True
    )
    ratio = slices // groups
    span = slices // ratio
    half = me_t // span
    pick_half = (jnp.arange(ratio) == half)[None, :, None, None]
    outgoing = jnp.where(pick_half, mine[:, None], jnp.zeros((), BF16)).reshape(slices, cap, narrow)
    incoming = lax.all_to_all(outgoing, "tp", split_axis=0, concat_axis=0, tiled=True)
    take_from = lax.dynamic_slice_in_dim(incoming, me_t % ratio * span, span, 0)
    summed_out = take_from.transpose(1, 0, 2).reshape(cap, feat).astype(F32)
    bounds = cu_seqlens[0]
    live_count = bounds[SEQS]
    mixed = (tokens.astype(F32) + summed_out).astype(BF16)
    mixed = jnp.where((slots < live_count)[:, None], mixed, jnp.zeros((), BF16))
    member = (slots[None, :] >= bounds[:-1, None]) & (slots[None, :] < bounds[1:, None])
    seq_sums = jnp.dot(member.astype(BF16), mixed, preferred_element_type=F32)
    lengths = (bounds[1:] - bounds[:-1]).astype(F32)
    return (mixed, seq_sums / lengths[:, None])


def solution(mesh):
    placed = (
        P("fsdp", "tp"),
        P(),
        P(None, "tp"),
        P(None, "tp"),
        P("tp", None),
        P(("fsdp", "tp"), None),
        P(("fsdp", "tp"), None),
        P(("fsdp", "tp"), None),
        P(("fsdp", "tp"), None),
        P(None, ("fsdp", "tp")),
        P(None, ("fsdp", "tp")),
        P("fsdp", None),
    )
    return jax.shard_map(
        shards,
        mesh=mesh,
        in_specs=placed,
        out_specs=(P("fsdp", "tp"), P("fsdp", "tp")),
        check_vma=False,
    )
```

profile of v0, /device:TPU:0, one launch (start us, length us, event | category | flops | bytes accessed | tf_op | source)
XLA Modules:
  0.0 536.5 jit_solution(2134350978414402686)
XLA Ops:
  9.3 5.2 all-to-all-start
  15.2 11.8 %all-to-all-done = bf16[8,96,512]{2,1,0:T(8,128)(2,1)S(1)} async-done(((bf16[8,96,512]{2,1,0:T(8,128)(2,1)}), bf16[8,96,512]{2,1,0:T(8,128)(2,1)S(1)}, u32[]{:S(2)}, u32[]{:S(2)}) %all-to-all-start) | async-done | bytes 786464 | tf_op jit(solution)/shard_map/all_to_all | solution.py:60
  32.6 22.1 %all_to_all.135 = bf16[96,4,1024]{2,0,1:T(8,128)(2,1)} all-to-all(bf16[96,4,1024]{2,0,1:T(8,128)(2,1)S(1)} %copy.58), channel_id=1, replica_groups=mesh['fsdp'=4,'tp'=8] {'fsdp'}, dimensions={1} | all-to-all | bytes 1572864 | tf_op jit(solution)/shard_map/all_to_all | solution.py:26
  55.4 4.8 all-to-all-start.3
  65.2 4.6 all-to-all-start.2
  69.9 9.2 %all-gather = s32[4,1,9]{2,1,0:T(1,128)S(1)} all-gather(s32[1,1,9]{2,1,0:T(1,128)S(1)} %bitcast.123), channel_id=1, replica_groups=mesh['fsdp'=4,'tp'=8] {'fsdp'}, dimensions={0}, use_global_device_ids=true | all-gather | bytes 180 | tf_op jit(solution)/shard_map/all_gather | solution.py:66
  81.3 2.9 copy.73
  87.7 34.9 %all-to-all-done.2 = bf16[128,8,1536]{0,2,1:T(8,128)(2,1)} async-done(((bf16[128,8,1536]{0,2,1:T(8,128)(2,1)}), bf16[128,8,1536]{0,2,1:T(8,128)(2,1)}, u32[]{:S(2)}, u32[]{:S(2)}) %all-to-all-start.2) | async-done | bytes 3145760 | tf_op jit(solution)/shard_map/all_to_all | solution.py:26
  122.6 3.9 fusion.7
  126.6 12.5 %fusion.10 = bf16[1536,1024]{1,0:T(8,128)(2,1)S(1)} fusion(bf16[3072,1024]{1,0:T(8,128)(2,1)} %all-gather.4.cloned.1.call-done, s32[1536]{0:T(1024)S(1)} %fusion.27), kind=kOutput, calls=%fused_computation.20 | convolution fusion | flops 9669967872 | bytes 9443328 | tf_op jit(solution)/shard_map/dot_general | solution.py:78
  140.8 6.9 %convolution_convert_fusion.1 = bf16[1536,1536]{1,0:T(8,128)(2,1)} fusion(bf16[1536,1024]{1,0:T(8,128)(2,1)S(1)} %fusion.10, bf16[1024,1536]{0,1:T(8,128)(2,1)S(1)} %fusion.7), kind=kOutput, calls=%fused_computation.7 | convolution fusion | flops 4834197504 | bytes 11010048 | tf_op jit(solution)/shard_map/dot_general | solution.py:83
  149.1 3.4 all-to-all-start.5
  157.4 4.5 all-to-all-start.4
  164.3 2.9 copy.74
  167.2 32.5 %all-to-all-done.4 = bf16[128,8,1536]{0,2,1:T(8,128)(2,1)} async-done(((bf16[128,8,1536]{0,2,1:T(8,128)(2,1)}), bf16[128,8,1536]{0,2,1:T(8,128)(2,1)}, u32[]{:S(2)}, u32[]{:S(2)}) %all-to-all-start.4) | async-done | bytes 3145760 | tf_op jit(solution)/shard_map/all_to_all | solution.py:26
  199.8 4.0 fusion.5
  203.8 6.9 %convolution_convert_fusion = bf16[1536,1536]{1,0:T(8,128)(2,1)} fusion(bf16[1536,1024]{1,0:T(8,128)(2,1)S(1)} %copy-done.9, bf16[1024,1536]{0,1:T(8,128)(2,1)S(1)} %fusion.5), kind=kOutput, calls=%fused_computation.6 | convolution fusion | flops 4834197504 | bytes 11010048 | tf_op jit(solution)/shard_map/dot_general | solution.py:84
  211.5 7.4 %all_to_all.136 = f32[8,12,128]{2,1,0:T(8,128)S(1)} all-to-all(f32[8,12,128]{2,1,0:T(8,128)S(1)} %all_to_all.119), channel_id=1, replica_groups=mesh['fsdp'=4,'tp'=8] {'tp'}, dimensions={0} | all-to-all | bytes 98304 | tf_op jit(solution)/shard_map/all_to_all | solution.py:30
  218.9 3.7 all-to-all-start.6
  222.7 37.7 %all-to-all-done.6 = bf16[8,1536,128]{2,1,0:T(8,128)(2,1)S(1)} async-done(((bf16[8,1536,128]{2,1,0:T(8,128)(2,1)}), bf16[8,1536,128]{2,1,0:T(8,128)(2,1)S(1)}, u32[]{:S(2)}, u32[]{:S(2)}) %all-to-all-start.6) | async-done | bytes 3145760 | tf_op jit(solution)/shard_map/all_to_all | solution.py:30
  262.5 58.8 %reduce-scatter.8.cloned.1.call-done = bf16[384,1536]{1,0:T(8,128)(2,1)} async-done(((bf16[1536,1536]{1,0:T(8,128)(2,1)}), bf16[384,1536]{1,0:T(8,128)(2,1)}) %reduce-scatter.8.cloned.1.call-update) | async-done | bytes 1179664 | tf_op jit(solution)/shard_map/reduce_scatter | solution.py:87
  321.3 3.4 fusion.16
  324.8 5.1 fusion.9
  329.9 84.9 %all-gather.6.cloned.1.call-done = bf16[1536,1536]{1,0:T(8,128)(2,1)} async-done(((bf16[384,1536]{1,0:T(8,128)(2,1)}), bf16[1536,1536]{1,0:T(8,128)(2,1)}) %all-gather.6.cloned.1.call-update) | async-done | bytes 4718608 | tf_op jit(solution)/shard_map/all_gather | solution.py:93
  414.8 8.1 %convolution_convert_fusion.2 = bf16[1536,1024]{1,0:T(8,128)(2,1)S(1)} fusion(bf16[1536,1536]{1,0:T(8,128)(2,1)} %all-gather.6.cloned.1.call-done, bf16[1536,1024]{1,0:T(8,128)(2,1)} %fusion.9), kind=kOutput, calls=%fused_computation.19 | convolution fusion | flops 4833411072 | bytes 11010048 | tf_op jit(solution)/shard_map/dot_general | solution.py:96
  422.9 3.0 copy.71
  426.0 44.5 %reduce-scatter.10.cloned.1.call-done = bf16[128,1536]{1,0:T(8,128)(2,1)} async-done(((bf16[1024,1536]{1,0:T(8,128)(2,1)}), bf16[128,1536]{1,0:T(8,128)(2,1)}) %reduce-scatter.10.cloned.1.call-update) | async-done | bytes 393232
  470.5 5.5 %fusion.11 = bf16[3008,128]{1,0:T(8,128)(2,1)} fusion(s32[3008]{0:T(1024)S(1)} %select_n.86, bf16[128,1536]{1,0:T(8,128)(2,1)} %reduce-scatter.10.cloned.1.call-done), kind=kOutput, calls=%fused_computation.21 | convolution fusion | flops 1187799040 | bytes 1175296 | tf_op jit(solution)/shard_map/dot_general | solution.py:103
  476.0 4.7 all-to-all-start.8
  480.9 19.5 %all-to-all-done.8 = bf16[4,752,128]{2,1,0:T(8,128)(2,1)S(1)} async-done(((bf16[4,752,128]{2,1,0:T(8,128)(2,1)}), bf16[4,752,128]{2,1,0:T(8,128)(2,1)S(1)}, u32[]{:S(2)}, u32[]{:S(2)}) %all-to-all-start.8) | async-done | bytes 770080 | tf_op jit(solution)/shard_map/all_to_all | solution.py:104
  501.7 3.6 all-to-all-start.9
  507.8 18.0 %all-to-all-done.9 = bf16[8,752,128]{2,1,0:T(8,128)(2,1)S(1)} async-done(((bf16[8,752,128]{2,1,0:T(8,128)(2,1)}), bf16[8,752,128]{2,1,0:T(8,128)(2,1)S(1)}, u32[]{:S(2)}, u32[]{:S(2)}) %all-to-all-start.9) | async-done | bytes 1540128 | tf_op jit(solution)/shard_map/all_to_all | solution.py:112
  (85 shorter events, 41.5 us)
Async XLA Ops:
  9.3 17.8 %all-to-all-start = ((bf16[8,96,512]{2,1,0:T(8,128)(2,1)}), bf16[8,96,512]{2,1,0:T(8,128)(2,1)S(1)}, u32[]{:S(2)}, u32[]{:S(2)}) async-start(bf16[8,96,512]{2,1,0:T(8,128)(2,1)} %bitcast.7), calls=%async_computation | async-start | bytes 1572864 | tf_op jit(solution)/shard_map/all_to_all | solution.py:60
  14.5 112.1 %all-gather.4.cloned.1.call-start = ((), (), s32[]{:S(2)}) async-start(), calls=%async_computation.13 | async-start | bytes 7077888 | tf_op jit(solution)/shard_map/all_gather | solution.py:65
  30.3 24.4 %copy-start.4 = (f32[128,96]{0,1:T(8,128)S(1)}, f32[128,96]{0,1:T(8,128)}, u32[]{:S(2)}) copy-start(f32[128,96]{0,1:T(8,128)} %param.19) | copy-start | bytes 147460
  30.4 29.8 %copy-start.1 = (bf16[128,12288]{1,0:T(8,128)(2,1)S(1)}, bf16[128,12288]{1,0:T(8,128)(2,1)}, u32[]{:S(2)}) copy-start(bf16[128,12288]{1,0:T(8,128)(2,1)} %param.17) | copy-start | bytes 9437188
  55.4 9.8 %all-to-all-start.3 = ((f32[128,8,12]{0,2,1:T(8,128)}), f32[128,8,12]{0,2,1:T(8,128)S(1)}, u32[]{:S(2)}, u32[]{:S(2)}) async-start(f32[128,8,12]{0,2,1:T(8,128)} %all_to_all.107), calls=%async_computation.3 | async-start | bytes 131072 | tf_op jit(solution)/shard_map/all_to_all | solution.py:26
  65.2 4.7 copy-start.7
  65.2 57.4 %all-to-all-start.2 = ((bf16[128,8,1536]{0,2,1:T(8,128)(2,1)}), bf16[128,8,1536]{0,2,1:T(8,128)(2,1)}, u32[]{:S(2)}, u32[]{:S(2)}) async-start(bf16[128,8,1536]{0,2,1:T(8,128)(2,1)} %bitcast.11), calls=%async_computation.2 | async-start | bytes 6291456 | tf_op jit(solution)/shard_map/all_to_all | solution.py:26
  69.8 192.6 %reduce-scatter.6.cloned.1.call-start = ((), (), s32[]{:S(2)}) async-start(), calls=%async_computation.14 | async-start | bytes 5898240 | tf_op jit(solution)/shard_map/reduce_scatter | solution.py:86
  139.1 1.6 copy-start.8
  147.7 0.8 copy-start.5
  147.7 4.8 copy-start.2
  149.1 8.3 %all-to-all-start.5 = ((f32[128,8,12]{0,2,1:T(8,128)}), f32[128,8,12]{0,2,1:T(8,128)S(1)}, u32[]{:S(2)}, u32[]{:S(2)}) async-start(f32[128,8,12]{0,2,1:T(8,128)} %all_to_all.112), calls=%async_computation.6 | async-start | bytes 131072 | tf_op jit(solution)/shard_map/all_to_all | solution.py:26
  157.4 42.4 %all-to-all-start.4 = ((bf16[128,8,1536]{0,2,1:T(8,128)(2,1)}), bf16[128,8,1536]{0,2,1:T(8,128)(2,1)}, u32[]{:S(2)}, u32[]{:S(2)}) async-start(bf16[128,8,1536]{0,2,1:T(8,128)(2,1)} %bitcast.15), calls=%async_computation.5 | async-start | bytes 6291456 | tf_op jit(solution)/shard_map/all_to_all | solution.py:26
  161.9 159.4 %reduce-scatter.8.cloned.1.call-start = ((), (), s32[]{:S(2)}) async-start(), calls=%async_computation.15 | async-start | bytes 5898240 | tf_op jit(solution)/shard_map/reduce_scatter | solution.py:87
  199.8 4.0 copy-start.9
  210.7 0.8 copy-start.6
  218.9 41.4 %all-to-all-start.6 = ((bf16[8,1536,128]{2,1,0:T(8,128)(2,1)}), bf16[8,1536,128]{2,1,0:T(8,128)(2,1)S(1)}, u32[]{:S(2)}, u32[]{:S(2)}) async-start(bf16[8,1536,128]{2,1,0:T(8,128)(2,1)} %bitcast.108), calls=%async_computation.8 | async-start | bytes 6291456 | tf_op jit(solution)/shard_map/all_to_all | solution.py:30
  222.5 192.2 %all-gather.6.cloned.1.call-start = ((), (), s32[]{:S(2)}) async-start(), calls=%async_computation.16 | async-start | bytes 5898240 | tf_op jit(solution)/shard_map/all_gather | solution.py:93
  262.4 62.3 %copy-start = (bf16[1536,1024]{1,0:T(8,128)(2,1)S(1)}, bf16[1536,1024]{1,0:T(8,128)(2,1)}, u32[]{:S(2)}) copy-start(bf16[1536,1024]{1,0:T(8,128)(2,1)} %copy_bitcast_fusion) | copy-start | bytes 9437188
  324.7 145.8 %reduce-scatter.10.cloned.1.call-start = ((), (), s32[]{:S(2)}) async-start(), calls=%async_computation.17 | async-start | bytes 3538944
  476.0 29.2 %copy-start.3 = (bf16[752,512]{1,0:T(8,128)(2,1)S(1)}, bf16[752,512]{1,0:T(8,128)(2,1)}, u32[]{:S(2)}) copy-start(bf16[752,512]{1,0:T(8,128)(2,1)} %param.12) | copy-start | bytes 2310148
  476.0 24.3 %all-to-all-start.8 = ((bf16[4,752,128]{2,1,0:T(8,128)(2,1)}), bf16[4,752,128]{2,1,0:T(8,128)(2,1)S(1)}, u32[]{:S(2)}, u32[]{:S(2)}) async-start(bf16[4,752,128]{2,1,0:T(8,128)(2,1)} %bitcast.23), calls=%async_computation.10 | async-start | bytes 1540096 | tf_op jit(solution)/shard_map/all_to_all | solution.py:104
  501.7 24.2 %all-to-all-start.9 = ((bf16[8,752,128]{2,1,0:T(8,128)(2,1)}), bf16[8,752,128]{2,1,0:T(8,128)(2,1)S(1)}, u32[]{:S(2)}, u32[]{:S(2)}) async-start(bf16[8,752,128]{2,1,0:T(8,128)(2,1)} %bitcast_select_fusion), calls=%async_computation.11 | async-start | bytes 3080192 | tf_op jit(solution)/shard_map/all_to_all | solution.py:112
Sparse Core Ops, SparseCore 0:
  54.9 71.6 all-gather.3
  147.8 85.2 reduce-scatter.5
  235.4 85.7 reduce-scatter.7
  324.8 89.8 all-gather.5
  426.0 44.4 reduce-scatter.9
where the time goes:
time: 538 us; the launch traced here: 536 us
  waiting for transfers between devices  347 us (64%)
  matrix products  40.9 us (8%)
  blocking collectives  38.7 us (7%)
  local copies, waits for them, and re-layouts  35.5 us (7%)
  starting transfers between devices  34.8 us (6%)
  other arithmetic  25.4 us (5%)
  between operations  14.1 us (3%)
    all_gather x1, waiting for transfers between devices, shards(): hidden_all = lax.all_gather(hidden, 'fsdp', axis=0, tiled=True)  84.9 us
    all_to_all x4, waiting for transfers between devices, swap_up(): lax.all_to_all(part, axis_name, split_axis=1, concat_axis=0, tiled=True)  71.8 us
    reduce_scatter x1, waiting for transfers between devices, shards(): up_sum = lax.psum_scatter(up_part, 'fsdp', scatter_dimension=0, tiled=True)  58.8 us
    unnamed x6, waiting for transfers between devices  44.5 us
    all_to_all x1, waiting for transfers between devices, swap_down(): return lax.all_to_all(part, 'tp', split_axis=0, concat_axis=1, tiled=True)  37.7 us
    all_to_all x1, blocking collectives, swap_up(): lax.all_to_all(part, axis_name, split_axis=1, concat_axis=0, tiled=True)  22.1 us
    unnamed x33, local copies, waits for them, and re-layouts  20 us
    all_to_all x1, waiting for transfers between devices, shards(): lax.all_to_all(placed_rows.reshape(groups, cap, narrow), 'fsdp', split_ax...  19.5 us
  transfers between devices with their start and end apart: 13, of which 12 were waited for; matrix products, arithmetic and copies ran while one was open for 8% of the time, Pallas kernels for 0%

commit v1 on v0

--- a/solution.py
+++ b/solution.py
@@ -90,7 +90,12 @@
         (gate_sum, up_sum, down_codes, down_scales)
     )
     hidden = (jax.nn.silu(gate_sum.astype(F32)) * up_sum.astype(F32)).astype(BF16)
-    hidden_all = lax.all_gather(hidden, "fsdp", axis=0, tiled=True)
+    ring = [hidden]
+    for hop in range(3):
+        ring.append(lax.ppermute(ring[-1], "fsdp", [(dev, (dev + 1) % 4) for dev in range(4)]))
+    hidden_all = jnp.roll(
+        jnp.concatenate(ring[::-1], axis=0), (lax.axis_index("fsdp") + 1) * ring[0].shape[0], axis=0
+    )
     down_cols = lax.dynamic_slice_in_dim(base_down, me_f * depth, depth, 1)
     w_down = dequant_cols(down_cols, down_codes, down_scales)
     out_part = jnp.dot(hidden_all, w_down, preferred_element_type=F32).astype(BF16)

time: 538 us -> 538 us (level)
  local copies, waits for them, and re-layouts: 35.5 us -> 43.3 us
    all_gather x1 -> x0, waiting for transfers between devices: 84.9 us -> none  [shards(): hidden_all = lax.all_gather(hidden, 'fsdp', axis=0, tiled=True)]
    ppermute x0 -> x3, waiting for transfers between devices: none -> 81.2 us  [shards(): lax.ppermute(ring[-1], 'fsdp', [(dev, (dev + 1) % 4) for dev in range(4)])]
    unnamed x33 -> x48, local copies, waits for them, and re-layouts: 20 us -> 27.7 us
    unnamed x6 -> x5, waiting for transfers between devices: 44.5 us -> 44.3 us
  transfers between devices with their start and end apart: 13 -> 15, of which waited for: 12 -> 14; matrix products, arithmetic and copies ran while one was open for 8% -> 8% of each run, Pallas kernels for 0% -> 0%
where the time goes in v1:
time: 538 us; the launch traced here: 536 us
  waiting for transfers between devices  343 us (64%)
  local copies, waits for them, and re-layouts  43.3 us (8%)
  blocking collectives  38.7 us (7%)
  matrix products  38.1 us (7%)
  starting transfers between devices  36.3 us (7%)
  other arithmetic  22.8 us (4%)
  between operations  14.2 us (3%)
    ppermute x3, waiting for transfers between devices, shards(): lax.ppermute(ring[-1], 'fsdp', [(dev, (dev + 1) % 4) for dev in range(4)])  81.2 us
    all_to_all x4, waiting for transfers between devices, swap_up(): lax.all_to_all(part, axis_name, split_axis=1, concat_axis=0, tiled=True)  71.6 us
    reduce_scatter x1, waiting for transfers between devices, shards(): up_sum = lax.psum_scatter(up_part, 'fsdp', scatter_dimension=0, tiled=True)  58.8 us
    unnamed x5, waiting for transfers between devices  44.3 us
    all_to_all x1, waiting for transfers between devices, swap_down(): return lax.all_to_all(part, 'tp', split_axis=0, concat_axis=1, tiled=True)  37.7 us
    unnamed x48, local copies, waits for them, and re-layouts  27.7 us
    all_to_all x1, blocking collectives, swap_up(): lax.all_to_all(part, axis_name, split_axis=1, concat_axis=0, tiled=True)  22.1 us
    all_to_all x1, waiting for transfers between devices, shards(): lax.all_to_all(placed_rows.reshape(groups, cap, narrow), 'fsdp', split_ax...  19.5 us
  transfers between devices with their start and end apart: 15, of which 14 were waited for; matrix products, arithmetic and copies ran while one was open for 8% of the time, Pallas kernels for 0%

profile of v1, /device:TPU:0, one launch (start us, length us, event | category | flops | bytes accessed | tf_op | source)
XLA Modules:
  0.0 536.2 jit_solution(11191175972309176641)
XLA Ops:
  9.2 5.2 all-to-all-start
  15.2 11.8 %all-to-all-done = bf16[8,96,512]{2,1,0:T(8,128)(2,1)S(1)} async-done(((bf16[8,96,512]{2,1,0:T(8,128)(2,1)}), bf16[8,96,512]{2,1,0:T(8,128)(2,1)S(1)}, u32[]{:S(2)}, u32[]{:S(2)}) %all-to-all-start) | async-done | bytes 786464 | tf_op jit(solution)/shard_map/all_to_all | solution.py:60
  32.6 22.1 %all_to_all.135 = bf16[96,4,1024]{2,0,1:T(8,128)(2,1)} all-to-all(bf16[96,4,1024]{2,0,1:T(8,128)(2,1)S(1)} %copy.58), channel_id=1, replica_groups=mesh['fsdp'=4,'tp'=8] {'fsdp'}, dimensions={1} | all-to-all | bytes 1572864 | tf_op jit(solution)/shard_map/all_to_all | solution.py:26
  55.4 4.8 all-to-all-start.3
  65.2 4.6 all-to-all-start.2
  69.8 9.2 %all-gather = s32[4,1,9]{2,1,0:T(1,128)S(1)} all-gather(s32[1,1,9]{2,1,0:T(1,128)S(1)} %bitcast.122), channel_id=1, replica_groups=mesh['fsdp'=4,'tp'=8] {'fsdp'}, dimensions={0}, use_global_device_ids=true | all-gather | bytes 180 | tf_op jit(solution)/shard_map/all_gather | solution.py:66
  87.8 34.8 %all-to-all-done.2 = bf16[128,8,1536]{0,2,1:T(8,128)(2,1)} async-done(((bf16[128,8,1536]{0,2,1:T(8,128)(2,1)}), bf16[128,8,1536]{0,2,1:T(8,128)(2,1)}, u32[]{:S(2)}, u32[]{:S(2)}) %all-to-all-start.2) | async-done | bytes 3145760 | tf_op jit(solution)/shard_map/all_to_all | solution.py:26
  122.6 3.9 fusion.7
  126.6 12.5 %fusion.15 = bf16[1536,1024]{1,0:T(8,128)(2,1)S(1)} fusion(bf16[3072,1024]{1,0:T(8,128)(2,1)} %all-gather.3.cloned.1.call-done, s32[1536]{0:T(1024)S(1)} %fusion.32), kind=kOutput, calls=%fused_computation.22 | convolution fusion | flops 9669967872 | bytes 9443328 | tf_op jit(solution)/shard_map/dot_general | solution.py:78
  140.7 6.9 %convolution_convert_fusion.1 = bf16[1536,1536]{1,0:T(8,128)(2,1)} fusion(bf16[1536,1024]{1,0:T(8,128)(2,1)S(1)} %fusion.15, bf16[1024,1536]{0,1:T(8,128)(2,1)S(1)} %fusion.7), kind=kOutput, calls=%fused_computation.7 | convolution fusion | flops 4834197504 | bytes 11010048 | tf_op jit(solution)/shard_map/dot_general | solution.py:83
  149.0 3.4 all-to-all-start.5
  157.4 4.5 all-to-all-start.4
  164.2 2.9 copy.74
  167.2 32.5 %all-to-all-done.4 = bf16[128,8,1536]{0,2,1:T(8,128)(2,1)} async-done(((bf16[128,8,1536]{0,2,1:T(8,128)(2,1)}), bf16[128,8,1536]{0,2,1:T(8,128)(2,1)}, u32[]{:S(2)}, u32[]{:S(2)}) %all-to-all-start.4) | async-done | bytes 3145760 | tf_op jit(solution)/shard_map/all_to_all | solution.py:26
  199.7 4.0 fusion.5
  203.7 6.9 %convolution_convert_fusion = bf16[1536,1536]{1,0:T(8,128)(2,1)} fusion(bf16[1536,1024]{1,0:T(8,128)(2,1)S(1)} %copy-done.13, bf16[1024,1536]{0,1:T(8,128)(2,1)S(1)} %fusion.5), kind=kOutput, calls=%fused_computation.6 | convolution fusion | flops 4834197504 | bytes 11010048 | tf_op jit(solution)/shard_map/dot_general | solution.py:84
  211.5 7.4 %all_to_all.136 = f32[8,12,128]{2,1,0:T(8,128)S(1)} all-to-all(f32[8,12,128]{2,1,0:T(8,128)S(1)} %all_to_all.119), channel_id=1, replica_groups=mesh['fsdp'=4,'tp'=8] {'tp'}, dimensions={0} | all-to-all | bytes 98304 | tf_op jit(solution)/shard_map/all_to_all | solution.py:30
  218.8 3.7 all-to-all-start.6
  222.6 37.7 %all-to-all-done.6 = bf16[8,1536,128]{2,1,0:T(8,128)(2,1)S(1)} async-done(((bf16[8,1536,128]{2,1,0:T(8,128)(2,1)}), bf16[8,1536,128]{2,1,0:T(8,128)(2,1)S(1)}, u32[]{:S(2)}, u32[]{:S(2)}) %all-to-all-start.6) | async-done | bytes 3145760 | tf_op jit(solution)/shard_map/all_to_all | solution.py:30
  262.4 58.8 %reduce-scatter.8.cloned.1.call-done = bf16[384,1536]{1,0:T(8,128)(2,1)} async-done(((bf16[1536,1536]{1,0:T(8,128)(2,1)}), bf16[384,1536]{1,0:T(8,128)(2,1)}) %reduce-scatter.8.cloned.1.call-update) | async-done | bytes 1179664 | tf_op jit(solution)/shard_map/reduce_scatter | solution.py:87
  326.1 28.0 %collective-permute-done = bf16[384,1536]{1,0:T(8,128)(2,1)S(1)} collective-permute-done((bf16[384,1536]{1,0:T(8,128)(2,1)S(1)}, bf16[384,1536]{1,0:T(8,128)(2,1)S(1)}, u32[]{:S(2)}, u32[]{:S(2)}) %collective-permute-start) | collective-permute-done | bytes 1179680 | tf_op jit(solution)/shard_map/ppermute | solution.py:95
  355.1 28.7 %collective-permute-done.1 = bf16[384,1536]{1,0:T(8,128)(2,1)} collective-permute-done((bf16[384,1536]{1,0:T(8,128)(2,1)S(1)}, bf16[384,1536]{1,0:T(8,128)(2,1)}, u32[]{:S(2)}, u32[]{:S(2)}) %collective-permute-start.1) | collective-permute-done | bytes 1179680 | tf_op jit(solution)/shard_map/ppermute | solution.py:95
  383.8 3.4 fusion.9
  387.3 24.6 %collective-permute-done.2 = bf16[384,1536]{1,0:T(8,128)(2,1)} collective-permute-done((bf16[384,1536]{1,0:T(8,128)(2,1)}, bf16[384,1536]{1,0:T(8,128)(2,1)}, u32[]{:S(2)}, u32[]{:S(2)}) %collective-permute-start.2) | collective-permute-done | bytes 1179680 | tf_op jit(solution)/shard_map/ppermute | solution.py:95
  417.6 5.3 fusion.12
  422.9 3.0 copy.71
  426.0 44.2 %reduce-scatter.10.cloned.1.call-done = bf16[128,1536]{1,0:T(8,128)(2,1)} async-done(((bf16[1024,1536]{1,0:T(8,128)(2,1)}), bf16[128,1536]{1,0:T(8,128)(2,1)}) %reduce-scatter.10.cloned.1.call-update) | async-done | bytes 393232
  470.3 5.5 %fusion.16 = bf16[3008,128]{1,0:T(8,128)(2,1)} fusion(s32[3008]{0:T(1024)S(1)} %select_n.98, bf16[128,1536]{1,0:T(8,128)(2,1)} %reduce-scatter.10.cloned.1.call-done), kind=kOutput, calls=%fused_computation.23 | convolution fusion | flops 1187799040 | bytes 1175296 | tf_op jit(solution)/shard_map/dot_general | solution.py:108
  475.8 4.7 all-to-all-start.8
  480.6 19.5 %all-to-all-done.8 = bf16[4,752,128]{2,1,0:T(8,128)(2,1)S(1)} async-done(((bf16[4,752,128]{2,1,0:T(8,128)(2,1)}), bf16[4,752,128]{2,1,0:T(8,128)(2,1)S(1)}, u32[]{:S(2)}, u32[]{:S(2)}) %all-to-all-start.8) | async-done | bytes 770080 | tf_op jit(solution)/shard_map/all_to_all | solution.py:109
  501.5 3.6 all-to-all-start.9
  507.6 18.0 %all-to-all-done.9 = bf16[8,752,128]{2,1,0:T(8,128)(2,1)S(1)} async-done(((bf16[8,752,128]{2,1,0:T(8,128)(2,1)}), bf16[8,752,128]{2,1,0:T(8,128)(2,1)S(1)}, u32[]{:S(2)}, u32[]{:S(2)}) %all-to-all-start.9) | async-done | bytes 1540128 | tf_op jit(solution)/shard_map/all_to_all | solution.py:117
  (104 shorter events, 56.0 us)
Async XLA Ops:
  9.2 17.8 %all-to-all-start = ((bf16[8,96,512]{2,1,0:T(8,128)(2,1)}), bf16[8,96,512]{2,1,0:T(8,128)(2,1)S(1)}, u32[]{:S(2)}, u32[]{:S(2)}) async-start(bf16[8,96,512]{2,1,0:T(8,128)(2,1)} %bitcast.7), calls=%async_computation | async-start | bytes 1572864 | tf_op jit(solution)/shard_map/all_to_all | solution.py:60
  14.4 112.1 %all-gather.3.cloned.1.call-start = ((), (), s32[]{:S(2)}) async-start(), calls=%async_computation.13 | async-start | bytes 7077888 | tf_op jit(solution)/shard_map/all_gather | solution.py:65
  30.3 24.4 %copy-start.8 = (f32[128,96]{0,1:T(8,128)S(1)}, f32[128,96]{0,1:T(8,128)}, u32[]{:S(2)}) copy-start(f32[128,96]{0,1:T(8,128)} %param.19) | copy-start | bytes 147460
  30.3 29.8 %copy-start.5 = (bf16[128,12288]{1,0:T(8,128)(2,1)S(1)}, bf16[128,12288]{1,0:T(8,128)(2,1)}, u32[]{:S(2)}) copy-start(bf16[128,12288]{1,0:T(8,128)(2,1)} %param.17) | copy-start | bytes 9437188
  55.4 9.8 %all-to-all-start.3 = ((f32[128,8,12]{0,2,1:T(8,128)}), f32[128,8,12]{0,2,1:T(8,128)S(1)}, u32[]{:S(2)}, u32[]{:S(2)}) async-start(f32[128,8,12]{0,2,1:T(8,128)} %all_to_all.107), calls=%async_computation.3 | async-start | bytes 131072 | tf_op jit(solution)/shard_map/all_to_all | solution.py:26
  65.2 4.7 copy-start.11
  65.2 57.4 %all-to-all-start.2 = ((bf16[128,8,1536]{0,2,1:T(8,128)(2,1)}), bf16[128,8,1536]{0,2,1:T(8,128)(2,1)}, u32[]{:S(2)}, u32[]{:S(2)}) async-start(bf16[128,8,1536]{0,2,1:T(8,128)(2,1)} %bitcast.11), calls=%async_computation.2 | async-start | bytes 6291456 | tf_op jit(solution)/shard_map/all_to_all | solution.py:26
  69.8 192.6 %reduce-scatter.6.cloned.1.call-start = ((), (), s32[]{:S(2)}) async-start(), calls=%async_computation.14 | async-start | bytes 5898240 | tf_op jit(solution)/shard_map/reduce_scatter | solution.py:86
  139.1 1.6 copy-start.12
  147.6 0.8 copy-start.9
  147.6 4.8 copy-start.6
  149.0 8.3 %all-to-all-start.5 = ((f32[128,8,12]{0,2,1:T(8,128)}), f32[128,8,12]{0,2,1:T(8,128)S(1)}, u32[]{:S(2)}, u32[]{:S(2)}) async-start(f32[128,8,12]{0,2,1:T(8,128)} %all_to_all.112), calls=%async_computation.6 | async-start | bytes 131072 | tf_op jit(solution)/shard_map/all_to_all | solution.py:26
  157.4 42.4 %all-to-all-start.4 = ((bf16[128,8,1536]{0,2,1:T(8,128)(2,1)}), bf16[128,8,1536]{0,2,1:T(8,128)(2,1)}, u32[]{:S(2)}, u32[]{:S(2)}) async-start(bf16[128,8,1536]{0,2,1:T(8,128)(2,1)} %bitcast.15), calls=%async_computation.5 | async-start | bytes 6291456 | tf_op jit(solution)/shard_map/all_to_all | solution.py:26
  161.9 159.4 %reduce-scatter.8.cloned.1.call-start = ((), (), s32[]{:S(2)}) async-start(), calls=%async_computation.15 | async-start | bytes 5898240 | tf_op jit(solution)/shard_map/reduce_scatter | solution.py:87
  199.7 4.0 copy-start.13
  210.7 0.8 copy-start.10
  218.8 41.4 %all-to-all-start.6 = ((bf16[8,1536,128]{2,1,0:T(8,128)(2,1)}), bf16[8,1536,128]{2,1,0:T(8,128)(2,1)S(1)}, u32[]{:S(2)}, u32[]{:S(2)}) async-start(bf16[8,1536,128]{2,1,0:T(8,128)(2,1)} %bitcast.107), calls=%async_computation.8 | async-start | bytes 6291456 | tf_op jit(solution)/shard_map/all_to_all | solution.py:30
  222.5 247.8 %reduce-scatter.10.cloned.1.call-start = ((), (), s32[]{:S(2)}) async-start(), calls=%async_computation.16 | async-start | bytes 3538944
  262.4 121.4 %copy-start = (bf16[1536,1024]{1,0:T(8,128)(2,1)S(1)}, bf16[1536,1024]{1,0:T(8,128)(2,1)}, u32[]{:S(2)}) copy-start(bf16[1536,1024]{1,0:T(8,128)(2,1)} %copy_bitcast_fusion) | copy-start | bytes 9437188
  323.6 1.0 copy-start.1
  324.6 29.4 %collective-permute-start = (bf16[384,1536]{1,0:T(8,128)(2,1)S(1)}, bf16[384,1536]{1,0:T(8,128)(2,1)S(1)}, u32[]{:S(2)}, u32[]{:S(2)}) collective-permute-start(bf16[384,1536]{1,0:T(8,128)(2,1)S(1)} %fusion.21), channel_id=1, source_target_pairs={{0,8},{8,16},{16,24},{24,0},{1,9},{9,17},{17,25},{25,1},{2,10},{10... | collective-permute-start | bytes 3538952 | tf_op jit(solution)/shard_map/ppermute | solution.py:95
  354.1 1.0 copy-start.3
  355.1 28.7 %collective-permute-start.1 = (bf16[384,1536]{1,0:T(8,128)(2,1)S(1)}, bf16[384,1536]{1,0:T(8,128)(2,1)}, u32[]{:S(2)}, u32[]{:S(2)}) collective-permute-start(bf16[384,1536]{1,0:T(8,128)(2,1)S(1)} %collective-permute-done), channel_id=1, source_target_pairs={{0,8},{8,16},{16,24},{24,0},{1,9},{9,17},{17,25},{25,1},{2,10},{10... | collective-permute-start | bytes 3538952 | tf_op jit(solution)/shard_map/ppermute | solution.py:95
  383.8 28.0 %collective-permute-start.2 = (bf16[384,1536]{1,0:T(8,128)(2,1)}, bf16[384,1536]{1,0:T(8,128)(2,1)}, u32[]{:S(2)}, u32[]{:S(2)}) collective-permute-start(bf16[384,1536]{1,0:T(8,128)(2,1)} %collective-permute-done.1), channel_id=1, source_target_pairs={{0,8},{8,16},{16,24},{24,0},{1,9},{9,17},{17,25},{25,1},{2,10},{10... | collective-permute-start | bytes 3538952 | tf_op jit(solution)/shard_map/ppermute | solution.py:95
  387.2 27.3 %copy-start.4 = (bf16[384,1536]{1,0:T(8,128)(2,1)S(1)}, bf16[384,1536]{1,0:T(8,128)(2,1)}, u32[]{:S(2)}) copy-start(bf16[384,1536]{1,0:T(8,128)(2,1)} %copy-done.3) | copy-start | bytes 3538948
  387.2 27.4 %copy-start.2 = (bf16[384,1536]{1,0:T(8,128)(2,1)S(1)}, bf16[384,1536]{1,0:T(8,128)(2,1)}, u32[]{:S(2)}) copy-start(bf16[384,1536]{1,0:T(8,128)(2,1)} %copy-done.1) | copy-start | bytes 3538948
  475.8 29.3 %copy-start.7 = (bf16[752,512]{1,0:T(8,128)(2,1)S(1)}, bf16[752,512]{1,0:T(8,128)(2,1)}, u32[]{:S(2)}) copy-start(bf16[752,512]{1,0:T(8,128)(2,1)} %param.12) | copy-start | bytes 2310148
  475.8 24.3 %all-to-all-start.8 = ((bf16[4,752,128]{2,1,0:T(8,128)(2,1)}), bf16[4,752,128]{2,1,0:T(8,128)(2,1)S(1)}, u32[]{:S(2)}, u32[]{:S(2)}) async-start(bf16[4,752,128]{2,1,0:T(8,128)(2,1)} %bitcast.23), calls=%async_computation.10 | async-start | bytes 1540096 | tf_op jit(solution)/shard_map/all_to_all | solution.py:109
  501.5 24.2 %all-to-all-start.9 = ((bf16[8,752,128]{2,1,0:T(8,128)(2,1)}), bf16[8,752,128]{2,1,0:T(8,128)(2,1)S(1)}, u32[]{:S(2)}, u32[]{:S(2)}) async-start(bf16[8,752,128]{2,1,0:T(8,128)(2,1)} %bitcast_select_fusion), calls=%async_computation.11 | async-start | bytes 3080192 | tf_op jit(solution)/shard_map/all_to_all | solution.py:117
Sparse Core Ops, SparseCore 0:
  54.9 71.6 all-gather.2
  147.8 85.2 reduce-scatter.5
  235.4 85.7 reduce-scatter.7
  426.0 44.2 reduce-scatter.9
